TPU v7x, 32 devices: a whole 2x2x4 slice. The times are simulated.
32 devices in a mesh: slab: 8 (over z, x), cross: 4 (over y, core).
Axes of the slice: x: 2, y: 2, z: 4, core: 2. Of those that a mesh axis runs over, the one named last changes fastest.
Arguments:
- gas_state: float32 [16, 64, 8192], P(None, 'slab', 'cross'), may hold values from -4 to 4, as said below
- parcel_record: float32 [5, 131072], P(None, ('slab', 'cross')), may hold values from -4 to 4, as said below
- condensed_shares: float32 [12, 131072], P(None, ('slab', 'cross')), may hold values from 0.02 to 0.2
- surface_steam_factor: float32 [12], replicated, may hold values from 0.2 to 2
- fine_cell: int32 [131072], P(('slab', 'cross')), may hold values from 0 to 20479, as said below
- block_counts: int32 [1024], P(('slab', 'cross')), may hold values from 16 to 128, as said below
Outputs:
- parcel_next: float32 [5, 131072], P(None, ('slab', 'cross'))
- fine_source: float32 [16, 64, 8192], P(None, 'slab', 'cross')
- correction: float32 [64, 4096], replicated
Inputs may be any that keep to these rules, and one draw needn't show every extreme that they name: fine_cell is plane * 2048 + k, with plane 0 and 9 the neighbouring slabs' last and first planes; it never points outside the gas mesh, and is non-decreasing over each device's 4096 slots. The live parcels of each aligned block of 128 slots are its first block_counts slots; the last block of each device's 4096 slots is full. `gas_state`: rows 0 to 2 velocity, row 3 temperature from 1 to 2, rows 4 on vapour fractions from 0 to 0.1. `parcel_record`: rows 0 to 2 velocity, row 3 temperature from 0.6 to 0.9, row 4 mass from 0.5 to 3.
All inputs are finite; a program needn't handle non-finite values.
Results may differ from a plain program's by a relative error of at most 0.00002.
Values sent between devices are 32-bit elements; how exact they have to be, the bound alone decides.
No kernel may reach another device: no remote copies, remote signals or barrier semaphores. Data moves between devices by JAX's collectives and lax.ppermute only.
A program may use at most 64 MiB of HBM per device.

v0:
```python
import jax
import jax.numpy as jnp
from jax import lax
from jax.sharding import PartitionSpec as P

BLOCK = 128
COARSE = 64
SWEEPS = 4
drag_rate = 0.5
evap_rate = 0.08
warming_speed = 0.3
latent_boiling_energy = 0.5
vapour_heat = 1.5
volume_inverse = 4.0


def with_halo(shard, sides, width):
    for axis, dim in sides:
        devices, length = (lax.axis_size(axis), shard.shape[dim])
        up = [(i, (i + 1) % devices) for i in range(devices - 1)]
        down = [(j, i) for i, j in up]
        last = lax.slice_in_dim(shard, length - width, length, axis=dim)
        leading = lax.slice_in_dim(shard, 0, width, axis=dim)
        before = lax.ppermute(last, axis, up)
        after = lax.ppermute(leading, axis, down)
        shard = jnp.concatenate([before, shard, after], axis=dim)
    return shard


def shifted(shard, axis, by):
    devices = lax.axis_size(axis)
    pairs = [(i, i + by) for i in range(devices) if 0 <= i + by < devices]
    return lax.ppermute(shard, axis, pairs)


def partner(shard, axis, bit):
    return lax.ppermute(shard, axis, [(i, i ^ 1 << bit) for i in range(lax.axis_size(axis))])


def advance(
    ambient_layer_fields, parcel_record, condensed_shares, surface_steam_factor, alive_mask
):
    gas_velocity = ambient_layer_fields[0:3]
    ambient_thermal_level = ambient_layer_fields[3]
    gas_vapour = ambient_layer_fields[4:]
    parcel_velocity = parcel_record[0:3]
    parcel_thermal_level = parcel_record[3]
    parcel_weight_amount = parcel_record[4]
    slip_velocity = gas_velocity - parcel_velocity
    slip_squared = jnp.sum(slip_velocity * slip_velocity, axis=0)
    drag_factor = (
        drag_rate
        * jnp.power(parcel_weight_amount, -2.0 / 3.0)
        * (1.0 + 0.15 * jnp.power(slip_squared + 1.0, 0.3435))
    )
    following_motion = (parcel_velocity + drag_factor * gas_velocity) / (1.0 + drag_factor)
    surface_steam_share = (
        condensed_shares
        * surface_steam_factor[:, None]
        * jnp.exp(2.0 * (parcel_thermal_level - 0.75))
    )
    species_rates = evap_rate * parcel_weight_amount * (surface_steam_share - gas_vapour)
    evaporated_weight = jnp.sum(species_rates, axis=0)
    thermal_exchange = (
        warming_speed
        * (ambient_thermal_level - parcel_thermal_level)
        * jnp.power(parcel_weight_amount, 1.0 / 3.0)
    )
    following_thermal_level = (
        parcel_thermal_level
        + (thermal_exchange - latent_boiling_energy * evaporated_weight) / parcel_weight_amount
    )
    following_weight = parcel_weight_amount - evaporated_weight
    momentum_terms = (
        parcel_weight_amount * (parcel_velocity - following_motion)
        + evaporated_weight * following_motion
    )
    energy_terms = vapour_heat * evaporated_weight - thermal_exchange
    source_terms = jnp.concatenate([momentum_terms, energy_terms[None], species_rates], axis=0)
    source_terms = source_terms * (alive_mask * volume_inverse)
    updated_parcel_record = jnp.concatenate(
        [following_motion, following_thermal_level[None], following_weight[None]], axis=0
    )
    parcel_next = jnp.where(alive_mask[None] > 0.5, updated_parcel_record, parcel_record)
    return (source_terms, parcel_next, evaporated_weight * alive_mask)


def neighbours(values_grid):
    edge = values_grid.shape[0]
    padded_x = jnp.pad(values_grid, ((1, 1), (0, 0)))
    summed = padded_x[2:] + padded_x[:-2]
    padded_y = jnp.pad(values_grid, ((0, 0), (edge, edge)))
    summed = summed + padded_y[:, 2 * edge :] + padded_y[:, : -2 * edge]
    padded_z = jnp.pad(values_grid, ((0, 0), (1, 1)))
    depth = jnp.arange(values_grid.shape[1], dtype=jnp.int32) % edge
    upper_mask = (depth < edge - 1).astype(values_grid.dtype)
    lower_mask = (depth > 0).astype(values_grid.dtype)
    return summed + padded_z[:, 2:] * upper_mask + padded_z[:, :-2] * lower_mask


def relax(coarse_source):
    solution = jnp.zeros_like(coarse_source)
    for sweep in range(SWEEPS):
        solution = (neighbours(solution) + coarse_source) / 6.0
    return solution


def body(gas_state, parcel_record, condensed_shares, surface_steam_factor, fine_cell, block_counts):
    fields = gas_state.shape[0]
    planes = gas_state.shape[1]
    cross_cells = gas_state.shape[2]
    slab_count = lax.axis_size("slab")
    cross_count = lax.axis_size("cross")
    slab_index = lax.axis_index("slab")
    padded_gas = with_halo(gas_state, (("slab", 1),), 1)
    gas_flat = padded_gas.reshape(fields, (planes + 2) * cross_cells)
    ambient_layer_fields = jnp.take(gas_flat, fine_cell, axis=1)
    slot_in_block = jnp.arange(BLOCK, dtype=jnp.int32)
    alive_mask = (slot_in_block[None, :] < block_counts[:, None]).reshape(-1).astype(jnp.float32)
    source_terms, parcel_next, evaporated_weight = advance(
        ambient_layer_fields, parcel_record, condensed_shares, surface_steam_factor, alive_mask
    )
    extended = (
        jnp.zeros((fields, (planes + 2) * cross_cells), jnp.float32)
        .at[:, fine_cell]
        .add(source_terms)
    )
    extended = extended.reshape(fields, planes + 2, cross_cells)
    from_above = shifted(extended[:, 0], "slab", -1)
    from_below = shifted(extended[:, planes + 1], "slab", 1)
    fine_source = extended[:, 1 : planes + 1]
    fine_source = fine_source.at[:, planes - 1].add(from_above)
    fine_source = fine_source.at[:, 0].add(from_below)
    squared = COARSE * COARSE
    fine_per_coarse = planes * slab_count // COARSE
    cross_per_coarse = cross_cells * cross_count // squared
    column_count = cross_cells // cross_per_coarse
    mass_cells = jnp.sum(fine_source[4:], axis=0) * (1.0 / volume_inverse)
    if fine_per_coarse <= planes:
        own_planes = planes // fine_per_coarse
        owned = mass_cells.reshape(own_planes, fine_per_coarse, column_count, cross_per_coarse)
        owned = jnp.sum(owned, axis=(1, 3)).reshape(-1)
    else:
        group = fine_per_coarse // planes
        owned = jnp.sum(mass_cells.reshape(planes, column_count, cross_per_coarse), axis=(0, 2))
        levels = group.bit_length() - 1
        for level in range(levels - 1, -1, -1):
            half = owned.shape[0] // 2
            upper_side = slab_index // 2**level % 2 == 1
            lower_part = owned[:half]
            upper_part = owned[half:]
            keep = jnp.where(upper_side, upper_part, lower_part)
            send = jnp.where(upper_side, lower_part, upper_part)
            owned = keep + partner(send, "slab", level)
    gathered = lax.all_gather(owned[None], ("slab", "cross"), axis=0, tiled=True)
    if fine_per_coarse <= planes:
        gathered = gathered.reshape(
            slab_count, cross_count, planes // fine_per_coarse, column_count
        )
        coarse_source = jnp.transpose(gathered, (0, 2, 1, 3)).reshape(COARSE, squared)
    else:
        group = fine_per_coarse // planes
        gathered = gathered.reshape(COARSE, group, cross_count, column_count // group)
        coarse_source = jnp.transpose(gathered, (0, 2, 1, 3)).reshape(COARSE, squared)
    correction = relax(coarse_source)
    return (parcel_next, fine_source, correction)


def solution(mesh):
    in_specs = (
        P(None, "slab", "cross"),
        P(None, ("slab", "cross")),
        P(None, ("slab", "cross")),
        P(),
        P(("slab", "cross")),
        P(("slab", "cross")),
    )
    out_specs = (P(None, ("slab", "cross")), P(None, "slab", "cross"), P())
    return jax.shard_map(body, mesh=mesh, in_specs=in_specs, out_specs=out_specs, check_vma=False)
```

profile of v0, /device:TPU:0, one launch (start us, length us, event | category | flops | bytes accessed | tf_op | source)
XLA Modules:
  0.0 172.7 jit_solution(5224186087210317424)
XLA Ops:
  7.2 2.0 %fusion.50 = (f32[16,1,2048]{2,1,0:T(1,128)S(1)}, f32[16,1,2048]{2,1,0:T(1,128)S(1)}) fusion(f32[16,8,2048]{2,1,0:T(8,128)} %param.10), kind=kLoop, calls=%fused_computation.91 | loop fusion | bytes 524288 | tf_op jit(solution)/shard_map/slice | solution.py:22
  9.2 4.9 %collective-permute-start = (f32[16,1,2048]{2,0,1:T(8,128)S(1)}, f32[16,1,2048]{2,0,1:T(8,128)S(1)}, u32[]{:S(2)}, u32[]{:S(2)}) collective-permute-start(f32[16,1,2048]{2,0,1:T(8,128)S(1)} %copy.117), channel_id=1, source_target_pairs={{0,4},{4,8},{8,12},{12,16},{16,20},{20,24},{24,28},{1,5},{5,9},{9,... | collective-permute-start | bytes 393224 | tf_op jit(solution)/shard_map/ppermute | solution.py:24
  14.2 1.3 collective-permute-start.1
  15.5 0.7 compare_select_fusion
  16.2 0.7 compare_and_fusion
  16.9 0.7 select_bitcast_fusion.1
  17.8 3.2 %collective-permute-done.1 = f32[16,1,2048]{2,0,1:T(8,128)S(1)} collective-permute-done((f32[16,1,2048]{2,0,1:T(8,128)S(1)}, f32[16,1,2048]{2,0,1:T(8,128)S(1)}, u32[]{:S(2)}, u32[]{:S(2)}) %collective-permute-start.1) | collective-permute-done | bytes 131104 | tf_op jit(solution)/shard_map/ppermute | solution.py:25
  21.2 0.4 pad_maximum_fusion
  21.6 5.4 %copy.107 = f32[16,10,2048]{0,2,1:T(8,128)} copy(f32[16,10,2048]{2,1,0:T(8,128)S(1)} %pad_maximum_fusion) | data formatting | bytes 2621440 | tf_op jit(solution)/shard_map/concatenate | solution.py:26
  27.0 14.8 %gather_fusion = f32[4096,16]{1,0:T(8,128)S(1)} fusion(f32[16,20480]{0,1:T(8,128)} %bitcast.39, s32[4096]{0:T(1024)S(1)} %get-tuple-element.61), kind=kCustom, calls=%fused_computation | custom fusion | bytes 540672 | tf_op jit(solution)/shard_map/jit(_take)/gather | solution.py:117
  41.8 0.6 copy.108
  43.2 0.6 copy.109
  43.8 26.9 %scatter_custom_fusion = f32[16,20480]{0,1:T(8,128)} fusion(s32[4096]{0:T(1024)S(1)} %get-tuple-element.60, f32[4096,16]{1,0:T(8,128)S(1)} %copy.109, f32[]{:T(128)} %constant.122.clone.1), kind=kCustom, calls=%fused_computation.2 | custom fusion | flops 65536 | bytes 1310724 | tf_op jit(solution)/shard_map/scatter-add | solution.py:126
  70.8 2.1 %fusion.49 = (f32[16,1,2048]{0,2,1:T(8,128)S(1)}, f32[16,1,2048]{0,2,1:T(8,128)S(1)}, f32[16,1,2048]{0,2,1:T(8,128)S(1)}) fusion(f32[16,10,2048]{0,2,1:T(8,128)} %bitcast.33), kind=kLoop, calls=%fused_computation.90 | loop fusion | bytes 786432 | tf_op jit(solution)/shard_map/slice | solution.py:130
  72.8 1.0 copy.121
  73.8 1.3 collective-permute-start.2
  75.1 7.3 %slice.196 = f32[16,8,2048]{0,2,1:T(8,128)} slice(f32[16,10,2048]{0,2,1:T(8,128)} %bitcast.34), slice={[0:16], [1:9], [0:2048]} | slice | bytes 2097152 | tf_op jit(solution)/shard_map/slice | solution.py:131
  82.4 5.1 %copy.119 = f32[16,8,2048]{2,0,1:T(8,128)S(1)} copy(f32[16,8,2048]{0,2,1:T(8,128)} %slice.196) | data formatting | bytes 2097152
  88.1 5.2 %collective-permute-start.3 = (f32[16,2048]{1,0:T(8,128)S(1)}, f32[16,2048]{1,0:T(8,128)S(1)}, u32[]{:S(2)}, u32[]{:S(2)}) collective-permute-start(f32[16,2048]{1,0:T(8,128)S(1)} %bitcast.44), channel_id=1, source_target_pairs={{0,4},{4,8},{8,12},{12,16},{16,20},{20,24},{24,28},{1,5},{5,9},{9,... | collective-permute-start | bytes 393224 | tf_op jit(solution)/shard_map/ppermute | solution.py:33
  93.3 0.9 fusion.35
  94.2 1.4 collective-permute-done.3
  96.2 1.3 reduce_sum.42
  97.7 0.7 reshape.210
  98.5 0.7 maximum_select_fusion
  99.3 1.6 copy.116
  100.8 54.9 %all-gather.3.cloned.1.call-done = f32[32,1,8192]{2,1,0:T(1,128)} async-done(((f32[1,1,8192]{2,1,0:T(1,128)}), f32[32,1,8192]{2,1,0:T(1,128)}) %all-gather.3.cloned.1.call-update) | async-done | bytes 1048592 | tf_op jit(solution)/shard_map/all_gather | solution.py:155
  155.8 3.8 %reduce.5 = f32[32,8192]{1,0:T(8,128)S(1)} reduce(f32[32,1,8192]{2,1,0:T(1,128)} %all-gather.3.cloned.1.call-done, f32[]{:T(128)} %constant.162), dimensions={1}, to_apply=%all-gather.reduce_sub_computation | reduce | bytes 2097156 | tf_op jit(solution)/shard_map/all_gather | solution.py:155
  159.6 0.6 copy.123
  160.3 1.1 fusion.28
  161.4 1.1 fusion.8
  162.6 1.1 fusion.15
  163.7 2.1 %fusion.22 = f32[64,4096]{1,0:T(8,128)} fusion(f32[64,4096]{1,0:T(8,128)S(1)} %bitcast.38, f32[64,4096]{1,0:T(8,128)S(1)} %fusion.15, f32[4096]{0:T(1024)S(1)} %get-tuple-element.63, f32[4096]{0:T(1024)S(1)} %get-tuple-element.62), kind=kLoop, calls=%fused_computation.37 | loop fusion | flops 2359296 | bytes 3178496 | tf_op jit(solution)/shard_map/div | solution.py:104
  (37 shorter events, 2.8 us)
Async XLA Ops:
  7.2 14.0 %copy-start = (f32[16,8,2048]{2,1,0:T(8,128)S(1)}, f32[16,8,2048]{2,1,0:T(8,128)}, u32[]{:S(2)}) copy-start(f32[16,8,2048]{2,1,0:T(8,128)} %param.10) | copy-start | bytes 3145732
  7.2 148.6 %all-gather.3.cloned.1.call-start = ((), (), s32[]{:S(2)}) async-start(), calls=%async_computation | async-start | bytes 1081344 | tf_op jit(solution)/shard_map/all_gather | solution.py:155
  9.2 8.4 %collective-permute-start = (f32[16,1,2048]{2,0,1:T(8,128)S(1)}, f32[16,1,2048]{2,0,1:T(8,128)S(1)}, u32[]{:S(2)}, u32[]{:S(2)}) collective-permute-start(f32[16,1,2048]{2,0,1:T(8,128)S(1)} %copy.117), channel_id=1, source_target_pairs={{0,4},{4,8},{8,12},{12,16},{16,20},{20,24},{24,28},{1,5},{5,9},{9,... | collective-permute-start | bytes 393224 | tf_op jit(solution)/shard_map/ppermute | solution.py:24
  14.2 6.9 %collective-permute-start.1 = (f32[16,1,2048]{2,0,1:T(8,128)S(1)}, f32[16,1,2048]{2,0,1:T(8,128)S(1)}, u32[]{:S(2)}, u32[]{:S(2)}) collective-permute-start(f32[16,1,2048]{2,0,1:T(8,128)S(1)} %copy.118), channel_id=1, source_target_pairs={{4,0},{8,4},{12,8},{16,12},{20,16},{24,20},{28,24},{5,1},{9,5},{13... | collective-permute-start | bytes 393224 | tf_op jit(solution)/shard_map/ppermute | solution.py:25
  27.0 15.4 %copy-start.1 = (f32[5,4096]{1,0:T(8,128)S(1)}, f32[5,4096]{1,0:T(8,128)}, u32[]{:S(2)}) copy-start(f32[5,4096]{1,0:T(8,128)} %param.11) | copy-start | bytes 245764
  41.8 1.0 copy-start.2
  41.8 0.9 copy-start.4
  73.8 19.5 %collective-permute-start.2 = (f32[16,2048]{1,0:T(8,128)}, f32[16,2048]{1,0:T(8,128)}, u32[]{:S(2)}, u32[]{:S(2)}) collective-permute-start(f32[16,2048]{1,0:T(8,128)} %bitcast.13), channel_id=1, source_target_pairs={{4,0},{8,4},{12,8},{16,12},{20,16},{24,20},{28,24},{5,1},{9,5},{13... | collective-permute-start | bytes 393224 | tf_op jit(solution)/shard_map/ppermute | solution.py:33
  88.1 7.5 %collective-permute-start.3 = (f32[16,2048]{1,0:T(8,128)S(1)}, f32[16,2048]{1,0:T(8,128)S(1)}, u32[]{:S(2)}, u32[]{:S(2)}) collective-permute-start(f32[16,2048]{1,0:T(8,128)S(1)} %bitcast.44), channel_id=1, source_target_pairs={{0,4},{4,8},{8,12},{12,16},{16,20},{20,24},{24,28},{1,5},{5,9},{9,... | collective-permute-start | bytes 393224 | tf_op jit(solution)/shard_map/ppermute | solution.py:33
  95.6 2.8 %copy-start.3 = (s32[32]{0:T(128)S(1)}, s32[32]{0:T(128)}, u32[]{:S(2)}) copy-start(s32[32]{0:T(128)} %param.15) | copy-start | bytes 388
Sparse Core Ops, SparseCore 0:
  98.5 57.2 all-gather.2
where the time goes:
time: 173 us
  waiting for transfers between devices  59.6 us (34%)
  local copies, waits for them, and re-layouts  43.2 us (25%)
  other arithmetic  43 us (25%)
  between operations  14.3 us (8%)
  starting transfers between devices  12.7 us (7%)
    all_gather x1, waiting for transfers between devices, body(): lax.all_gather(owned[None], ('slab', 'cross'), axis=0, tiled=True)  54.9 us
    scatter-add x1, other arithmetic, body(): extended = jnp.zeros((fields, (planes + 2) * cross_cells), jnp.float32).a...  26.9 us
    gather x2, local copies, waits for them, and re-layouts, body(): ambient_layer_fields = jnp.take(gas_flat, fine_cell, axis=1)  15.3 us
    unnamed x19, local copies, waits for them, and re-layouts  9.69 us
    slice x1, local copies, waits for them, and re-layouts, body(): fine_source = extended[:, 1:planes + 1]  7.3 us
    ppermute x2, starting transfers between devices, shifted(): return lax.ppermute(shard, axis, pairs)  6.45 us
    div x4, other arithmetic, relax(): solution = (neighbours(solution) + coarse_source) / 6.0  5.57 us
    concatenate x1, local copies, waits for them, and re-layouts, with_halo(): shard = jnp.concatenate([before, shard, after], axis=dim)  5.39 us
  transfers between devices with their start and end apart: 5, of which 3 were waited for; matrix products, arithmetic and copies ran while one was open for 11% of the time, Pallas kernels for 0%

commit v1 on v0

--- a/solution.py
+++ b/solution.py
@@ -106,6 +106,14 @@
 
 
 def body(gas_state, parcel_record, condensed_shares, surface_steam_factor, fine_cell, block_counts):
+
+    def lay_views(raw):
+        big = jnp.stack(lax.axis_size(("slab", "cross")) * [raw])
+        everything = jnp.concatenate(
+            lax.all_to_all(big, split_axis=0, concat_axis=0, axis_name=("slab", "cross")), 0
+        )
+        return everything
+
     fields = gas_state.shape[0]
     planes = gas_state.shape[1]
     cross_cells = gas_state.shape[2]
@@ -152,7 +160,7 @@
             keep = jnp.where(upper_side, upper_part, lower_part)
             send = jnp.where(upper_side, lower_part, upper_part)
             owned = keep + partner(send, "slab", level)
-    gathered = lax.all_gather(owned[None], ("slab", "cross"), axis=0, tiled=True)
+    gathered = lay_views(owned[None])
     if fine_per_coarse <= planes:
         gathered = gathered.reshape(
             slab_count, cross_count, planes // fine_per_coarse, column_count

time: 173 us -> 137 us (0.79)
  waiting for transfers between devices: 59.6 us -> 28.4 us
  between operations: 14.3 us -> 0.94 us
  starting transfers between devices: 12.7 us -> 20.8 us
    all_gather x1 -> x0, waiting for transfers between devices: 54.9 us -> none  [body(): lax.all_gather(owned[None], ('slab', 'cross'), axis=0, tiled=True)]
    all_to_all x0 -> x1, waiting for transfers between devices: none -> 23.6 us  [lay_views(): lax.all_to_all(big, split_axis=0, concat_axis=0, axis_name=('slab', 'cros...]
    all_to_all x0 -> x1, starting transfers between devices: none -> 8.32 us  [lay_views(): lax.all_to_all(big, split_axis=0, concat_axis=0, axis_name=('slab', 'cros...]
    all_gather x1 -> x0, other arithmetic: 3.8 us -> none  [body(): lax.all_gather(owned[None], ('slab', 'cross'), axis=0, tiled=True)]
    all_to_all x0 -> x1, other arithmetic: none -> 2.57 us  [lay_views(): lax.all_to_all(big, split_axis=0, concat_axis=0, axis_name=('slab', 'cros...]
    another operation x0 -> x1, local copies, waits for them, and re-layouts: none -> 1.92 us  [lay_views(): big = jnp.stack(lax.axis_size(('slab', 'cross')) * [raw])]
  transfers between devices with their start and end apart: 5 -> 5, of which waited for: 3 -> 3; matrix products, arithmetic and copies ran while one was open for 11% -> 14% of each run, Pallas kernels for 0% -> 0%
where the time goes in v1:
time: 137 us; the launch traced here: 136 us
  local copies, waits for them, and re-layouts  44.3 us (32%)
  other arithmetic  41.7 us (30%)
  waiting for transfers between devices  28.4 us (21%)
  starting transfers between devices  20.8 us (15%)
    scatter-add x1, other arithmetic, body(): extended = jnp.zeros((fields, (planes + 2) * cross_cells), jnp.float32).a...  27 us
    all_to_all x1, waiting for transfers between devices, lay_views(): lax.all_to_all(big, split_axis=0, concat_axis=0, axis_name=('slab', 'cros...  23.6 us
    gather x2, local copies, waits for them, and re-layouts, body(): ambient_layer_fields = jnp.take(gas_flat, fine_cell, axis=1)  15.3 us
    unnamed x19, local copies, waits for them, and re-layouts  9.02 us
    all_to_all x1, starting transfers between devices, lay_views(): lax.all_to_all(big, split_axis=0, concat_axis=0, axis_name=('slab', 'cros...  8.32 us
    slice x1, local copies, waits for them, and re-layouts, body(): fine_source = extended[:, 1:planes + 1]  7.31 us
    ppermute x2, starting transfers between devices, shifted(): return lax.ppermute(shard, axis, pairs)  6.27 us
    div x4, other arithmetic, relax(): solution = (neighbours(solution) + coarse_source) / 6.0  5.57 us
  transfers between devices with their start and end apart: 5, of which 3 were waited for; matrix products, arithmetic and copies ran while one was open for 14% of the time, Pallas kernels for 0%

profile of v1, /device:TPU:0, one launch (start us, length us, event | category | flops | bytes accessed | tf_op | source)
XLA Modules:
  0.0 136.1 jit_solution(6537845980183800069)
XLA Ops:
  0.6 1.8 %fusion.50 = (f32[16,1,2048]{2,1,0:T(1,128)S(1)}, f32[16,1,2048]{2,1,0:T(1,128)S(1)}) fusion(f32[16,8,2048]{2,1,0:T(8,128)} %param.10), kind=kLoop, calls=%fused_computation.92 | loop fusion | bytes 524288 | tf_op jit(solution)/shard_map/slice | solution.py:22
  2.5 4.9 %collective-permute-start = (f32[16,1,2048]{2,0,1:T(8,128)S(1)}, f32[16,1,2048]{2,0,1:T(8,128)S(1)}, u32[]{:S(2)}, u32[]{:S(2)}) collective-permute-start(f32[16,1,2048]{2,0,1:T(8,128)S(1)} %copy.117), channel_id=1, source_target_pairs={{0,4},{4,8},{8,12},{12,16},{16,20},{20,24},{24,28},{1,5},{5,9},{9,... | collective-permute-start | bytes 393224 | tf_op jit(solution)/shard_map/ppermute | solution.py:24
  7.4 1.3 collective-permute-start.1
  8.7 0.7 compare_select_fusion
  9.5 0.7 compare_and_fusion
  10.2 0.7 select_bitcast_fusion.1
  11.1 3.2 %collective-permute-done.1 = f32[16,1,2048]{2,0,1:T(8,128)S(1)} collective-permute-done((f32[16,1,2048]{2,0,1:T(8,128)S(1)}, f32[16,1,2048]{2,0,1:T(8,128)S(1)}, u32[]{:S(2)}, u32[]{:S(2)}) %collective-permute-start.1) | collective-permute-done | bytes 131104 | tf_op jit(solution)/shard_map/ppermute | solution.py:25
  14.8 5.4 %copy.107 = f32[16,10,2048]{0,2,1:T(8,128)} copy(f32[16,10,2048]{2,1,0:T(8,128)S(1)} %pad_maximum_fusion) | data formatting | bytes 2621440 | tf_op jit(solution)/shard_map/concatenate | solution.py:26
  20.2 14.8 %gather_fusion = f32[4096,16]{1,0:T(8,128)S(1)} fusion(f32[16,20480]{0,1:T(8,128)} %bitcast.43, s32[4096]{0:T(1024)S(1)} %get-tuple-element.61), kind=kCustom, calls=%fused_computation | custom fusion | bytes 540672 | tf_op jit(solution)/shard_map/jit(_take)/gather | solution.py:125
  35.1 0.6 copy.108
  36.5 0.6 copy.109
  37.1 27.0 %scatter_custom_fusion = f32[16,20480]{0,1:T(8,128)} fusion(s32[4096]{0:T(1024)S(1)} %get-tuple-element.60, f32[4096,16]{1,0:T(8,128)S(1)} %copy.109, f32[]{:T(128)} %constant.122.clone.1), kind=kCustom, calls=%fused_computation.2 | custom fusion | flops 65536 | bytes 1310724 | tf_op jit(solution)/shard_map/scatter-add | solution.py:134
  64.0 2.1 %fusion.49 = (f32[16,1,2048]{0,2,1:T(8,128)S(1)}, f32[16,1,2048]{0,2,1:T(8,128)S(1)}, f32[16,1,2048]{0,2,1:T(8,128)S(1)}) fusion(f32[16,10,2048]{0,2,1:T(8,128)} %bitcast.37), kind=kLoop, calls=%fused_computation.91 | loop fusion | bytes 786432 | tf_op jit(solution)/shard_map/slice | solution.py:138
  66.1 1.0 copy.121
  67.1 1.3 collective-permute-start.2
  68.3 7.3 %slice.196 = f32[16,8,2048]{0,2,1:T(8,128)} slice(f32[16,10,2048]{0,2,1:T(8,128)} %bitcast.38), slice={[0:16], [1:9], [0:2048]} | slice | bytes 2097152 | tf_op jit(solution)/shard_map/slice | solution.py:139
  75.7 5.1 %copy.119 = f32[16,8,2048]{2,0,1:T(8,128)S(1)} copy(f32[16,8,2048]{0,2,1:T(8,128)} %slice.196) | data formatting | bytes 2097152
  81.4 5.0 %collective-permute-start.3 = (f32[16,2048]{1,0:T(8,128)S(1)}, f32[16,2048]{1,0:T(8,128)S(1)}, u32[]{:S(2)}, u32[]{:S(2)}) collective-permute-start(f32[16,2048]{1,0:T(8,128)S(1)} %bitcast.48), channel_id=1, source_target_pairs={{0,4},{4,8},{8,12},{12,16},{16,20},{20,24},{24,28},{1,5},{5,9},{9,... | collective-permute-start | bytes 393224 | tf_op jit(solution)/shard_map/ppermute | solution.py:33
  86.4 0.9 fusion.35
  87.3 1.6 %collective-permute-done.3 = f32[16,2048]{1,0:T(8,128)S(1)} collective-permute-done((f32[16,2048]{1,0:T(8,128)S(1)}, f32[16,2048]{1,0:T(8,128)S(1)}, u32[]{:S(2)}, u32[]{:S(2)}) %collective-permute-start.3) | collective-permute-done | bytes 131104 | tf_op jit(solution)/shard_map/ppermute | solution.py:33
  89.5 1.3 reduce_sum.42
  91.0 1.9 %stack.3 = f32[32,1,8192]{2,1,0:T(1,128)} broadcast(f32[8192]{0:T(1024)S(1)} %bitcast.50), dimensions={2} | broadcast | bytes 1081344 | tf_op jit(solution)/shard_map/stack | solution.py:111
  92.9 8.3 %all-to-all-start = ((f32[32,1,8192]{2,1,0:T(1,128)}), f32[32,1,8192]{2,1,0:T(1,128)S(1)}, u32[]{:S(2)}, u32[]{:S(2)}) async-start(f32[32,1,8192]{2,1,0:T(1,128)} %stack.3), calls=%async_computation | async-start | bytes 2097152 | tf_op jit(solution)/shard_map/all_to_all | solution.py:113
  101.4 0.7 maximum_select_fusion
  102.1 1.6 %copy.116 = f32[16,8,2048]{2,1,0:T(8,128)} copy(f32[16,8,2048]{2,0,1:T(8,128)S(1)} %fusion.34) | data formatting | bytes 2097152
  103.7 23.6 %all-to-all-done = f32[32,1,8192]{2,1,0:T(1,128)S(1)} async-done(((f32[32,1,8192]{2,1,0:T(1,128)}), f32[32,1,8192]{2,1,0:T(1,128)S(1)}, u32[]{:S(2)}, u32[]{:S(2)}) %all-to-all-start) | async-done | bytes 1048608 | tf_op jit(solution)/shard_map/all_to_all | solution.py:113
  127.3 2.6 %reduce.5 = f32[32,8192]{1,0:T(8,128)S(1)} reduce(f32[32,1,8192]{2,1,0:T(1,128)S(1)} %all-to-all-done, f32[]{:T(128)} %constant.162), dimensions={1}, to_apply=%all_to_all.3.reduce_sub_computation | reduce | bytes 2097156 | tf_op jit(solution)/shard_map/all_to_all | solution.py:113
  129.8 0.6 copy.124
  130.5 1.1 fusion.28
  131.7 1.1 fusion.8
  132.8 1.1 fusion.15
  134.0 2.1 %fusion.22 = f32[64,4096]{1,0:T(8,128)} fusion(f32[64,4096]{1,0:T(8,128)S(1)} %bitcast.42, f32[64,4096]{1,0:T(8,128)S(1)} %fusion.15, f32[4096]{0:T(1024)S(1)} %get-tuple-element.63, f32[4096]{0:T(1024)S(1)} %get-tuple-element.62), kind=kLoop, calls=%fused_computation.37 | loop fusion | flops 2359296 | bytes 3178496 | tf_op jit(solution)/shard_map/div | solution.py:104
  (37 shorter events, 3.1 us)
Async XLA Ops:
  0.6 13.8 %copy-start = (f32[16,8,2048]{2,1,0:T(8,128)S(1)}, f32[16,8,2048]{2,1,0:T(8,128)}, u32[]{:S(2)}) copy-start(f32[16,8,2048]{2,1,0:T(8,128)} %param.10) | copy-start | bytes 3145732
  2.5 8.4 %collective-permute-start = (f32[16,1,2048]{2,0,1:T(8,128)S(1)}, f32[16,1,2048]{2,0,1:T(8,128)S(1)}, u32[]{:S(2)}, u32[]{:S(2)}) collective-permute-start(f32[16,1,2048]{2,0,1:T(8,128)S(1)} %copy.117), channel_id=1, source_target_pairs={{0,4},{4,8},{8,12},{12,16},{16,20},{20,24},{24,28},{1,5},{5,9},{9,... | collective-permute-start | bytes 393224 | tf_op jit(solution)/shard_map/ppermute | solution.py:24
  7.4 6.9 %collective-permute-start.1 = (f32[16,1,2048]{2,0,1:T(8,128)S(1)}, f32[16,1,2048]{2,0,1:T(8,128)S(1)}, u32[]{:S(2)}, u32[]{:S(2)}) collective-permute-start(f32[16,1,2048]{2,0,1:T(8,128)S(1)} %copy.118), channel_id=1, source_target_pairs={{4,0},{8,4},{12,8},{16,12},{20,16},{24,20},{28,24},{5,1},{9,5},{13... | collective-permute-start | bytes 393224 | tf_op jit(solution)/shard_map/ppermute | solution.py:25
  20.2 15.4 %copy-start.1 = (f32[5,4096]{1,0:T(8,128)S(1)}, f32[5,4096]{1,0:T(8,128)}, u32[]{:S(2)}) copy-start(f32[5,4096]{1,0:T(8,128)} %param.11) | copy-start | bytes 245764
  35.0 1.0 copy-start.2
  35.0 0.9 copy-start.4
  67.1 19.3 %collective-permute-start.2 = (f32[16,2048]{1,0:T(8,128)}, f32[16,2048]{1,0:T(8,128)}, u32[]{:S(2)}, u32[]{:S(2)}) collective-permute-start(f32[16,2048]{1,0:T(8,128)} %bitcast.13), channel_id=1, source_target_pairs={{4,0},{8,4},{12,8},{16,12},{20,16},{24,20},{28,24},{5,1},{9,5},{13... | collective-permute-start | bytes 393224 | tf_op jit(solution)/shard_map/ppermute | solution.py:33
  81.4 7.5 %collective-permute-start.3 = (f32[16,2048]{1,0:T(8,128)S(1)}, f32[16,2048]{1,0:T(8,128)S(1)}, u32[]{:S(2)}, u32[]{:S(2)}) collective-permute-start(f32[16,2048]{1,0:T(8,128)S(1)} %bitcast.48), channel_id=1, source_target_pairs={{0,4},{4,8},{8,12},{12,16},{16,20},{20,24},{24,28},{1,5},{5,9},{9,... | collective-permute-start | bytes 393224 | tf_op jit(solution)/shard_map/ppermute | solution.py:33
  90.8 10.5 %copy-start.3 = (s32[32]{0:T(128)S(1)}, s32[32]{0:T(128)}, u32[]{:S(2)}) copy-start(s32[32]{0:T(128)} %param.15) | copy-start | bytes 388
  92.9 34.4 %all-to-all-start = ((f32[32,1,8192]{2,1,0:T(1,128)}), f32[32,1,8192]{2,1,0:T(1,128)S(1)}, u32[]{:S(2)}, u32[]{:S(2)}) async-start(f32[32,1,8192]{2,1,0:T(1,128)} %stack.3), calls=%async_computation | async-start | bytes 2097152 | tf_op jit(solution)/shard_map/all_to_all | solution.py:113
